TPU v7x, 32 devices: a whole 2x2x4 slice. The times are simulated.
32 devices in a mesh: row: 4 (over x, core), col: 8 (over z, y).
Axes of the slice: x: 2, y: 2, z: 4, core: 2. Of those that a mesh axis runs over, the one named last changes fastest.
Arguments:
- normed: bfloat16 [12288, 6144], P(('row', 'col')), may hold values from -6 to 6
- out_grad: bfloat16 [12288, 6144], P(('row', 'col')), may hold values from -0.125 to 0.125
- w_in: bfloat16 [6144, 48], replicated, may hold values from -0.078125 to 0.078125
- hidden_grad: bfloat16 [12288, 48], P(('row', 'col')), may hold values from -0.125 to 0.125
- qkv_grad: bfloat16 [12288, 64], P(('row', 'col')), may hold values from -0.125 to 0.125
- bucket_order: int32 [160], replicated, may hold values from 0 to 159, each once
Outputs:
- buckets: bfloat16 [160, 6144], replicated
Inputs may be any that keep to these rules, and one draw needn't show every extreme that they name: bucket_order is a permutation of 0 to 159.
All inputs are finite; a program needn't handle non-finite values.
Results may differ from a plain program's by a relative error of at most 0.0044.
Values may be sent and summed in bfloat16 or wider, within the bound.
A program may use at most 64 MiB of HBM per device.

v0:
```python
import jax
import jax.numpy as jnp
from jax import lax
from jax.sharding import PartitionSpec as P

NB = 4


def local(normed, out_grad, w_in, hidden_grad, qkv_grad, bucket_order):
    pre = jnp.dot(normed, w_in, preferred_element_type=jnp.float32)
    cdf = 0.5 * (1.0 + lax.erf(pre * 0.7071067811865476))
    pdf = jnp.exp(-0.5 * pre * pre) * 0.3989422804014327
    hidden = (pre * cdf).astype(jnp.bfloat16)
    pre_grad = (hidden_grad.astype(jnp.float32) * (cdf + pre * pdf)).astype(jnp.bfloat16)
    grad_qkv = jnp.dot(qkv_grad.T, normed, preferred_element_type=jnp.float32)
    grad_in = jnp.dot(pre_grad.T, normed, preferred_element_type=jnp.float32)
    grad_out = jnp.dot(hidden.T, out_grad, preferred_element_type=jnp.float32)
    stacked = jnp.concatenate([grad_qkv, grad_in, grad_out], axis=0)
    ordered = jnp.take(stacked, bucket_order, axis=0)
    per_bucket = ordered.shape[0] // NB
    results = []
    for bucket in range(NB):
        piece = ordered[bucket * per_bucket : (bucket + 1) * per_bucket]
        summed = lax.psum(piece, ("row", "col")).astype(jnp.bfloat16)
        results.append(summed)
    return jnp.concatenate(results, axis=0)


def solution(mesh):
    in_specs = (
        P(("row", "col"), None),
        P(("row", "col"), None),
        P(),
        P(("row", "col"), None),
        P(("row", "col"), None),
        P(),
    )
    out_specs = P()
    return jax.shard_map(local, mesh=mesh, in_specs=in_specs, out_specs=out_specs, check_vma=False)
```

profile of v0, /device:TPU:1, one launch (start us, length us, event | category | flops | bytes accessed | tf_op | source)
XLA Modules:
  0.0 116.7 jit_solution(10145399101433720630)
XLA Ops:
  0.0 0.0 copy-start
  0.0 0.0 copy-start.2
  0.0 1.1 copy-done
  1.1 4.3 %fusion.15 = f32[384,48]{0,1:T(8,128)S(1)} fusion(bf16[384,6144]{1,0:T(8,128)(2,1)} %param.6, bf16[6144,48]{0,1:T(8,128)(2,1)S(1)} %copy-done), kind=kOutput, calls=%fused_computation.24 | convolution fusion | flops 226492416 | bytes 5382144 | tf_op jit(solution)/shard_map/dot_general | solution.py:10
  5.4 0.0 copy-done.2
  5.4 0.0 copy-start.1
  5.4 0.0 copy-start.4
  5.4 0.9 fusion.6
  6.4 1.4 %copy-done.1 = bf16[384,6144]{1,0:T(8,128)(2,1)S(1)} copy-done((bf16[384,6144]{1,0:T(8,128)(2,1)S(1)}, bf16[384,6144]{1,0:T(8,128)(2,1)}, u32[]{:S(2)}) %copy-start.1) | copy-done | bytes 4718616
  7.7 0.0 copy-done.4
  7.7 0.0 copy-start.3
  7.7 0.9 fusion.7
  8.7 0.0 copy-done.3
  8.7 0.9 fusion.14
  9.6 0.0 copy-start.5
  9.7 2.1 %pad_maximum_fusion = f32[160,6144]{1,0:T(8,128)} fusion(f32[48,6144]{1,0:T(8,128)S(1)} %fusion.6, f32[48,6144]{1,0:T(8,128)S(1)} %fusion.7, f32[64,6144]{1,0:T(8,128)S(1)} %fusion.14), kind=kLoop, calls=%fused_computation.1 | loop fusion | flops 1966080 | bytes 7864320 | tf_op jit(solution)/shard_map/concatenate | solution.py:18
  11.8 0.0 copy-done.5
  11.8 7.4 %gather_fusion = f32[160,6144]{1,0:T(8,128)} fusion(f32[160,6144]{1,0:T(8,128)} %pad_maximum_fusion, s32[1024]{0:T(1024)S(1)} %pad_clamp_fusion), kind=kCustom, calls=%fused_computation | custom fusion | bytes 7864960 | tf_op jit(solution)/shard_map/jit(_take)/gather | solution.py:19
  19.3 2.7 %broadcast_select_fusion = f32[160,6144]{1,0:T(8,128)S(1)} fusion(f32[160,6144]{1,0:T(8,128)} %gather_fusion, pred[160]{0:T(512)(128)(4,1)S(1)} %compare_and_fusion), kind=kLoop, calls=%fused_computation.3 | loop fusion | flops 983040 | bytes 7864480 | tf_op jit(solution)/shard_map/jit(_take)/select_n | solution.py:19
  22.0 1.2 %fusion.13 = (f32[40,6144]{1,0:T(8,128)S(1)}, f32[40,6144]{1,0:T(8,128)S(1)}, f32[40,6144]{1,0:T(8,128)S(1)}, f32[40,6144]{1,0:T(8,128)}) fusion(f32[160,6144]{1,0:T(8,128)S(1)} %broadcast_select_fusion), kind=kLoop, calls=%fused_computation.22 | loop fusion | bytes 7864320 | tf_op jit(solution)/shard_map/slice | solution.py:23
  23.2 90.6 %all-reduce.2 = (bf16[40,6144]{1,0:T(8,128)(2,1)}, bf16[40,6144]{1,0:T(8,128)(2,1)}, bf16[40,6144]{1,0:T(8,128)(2,1)}, bf16[40,6144]{1,0:T(8,128)(2,1)}) all-reduce(f32[40,6144]{1,0:T(8,128)S(1)} %get-tuple-element.10, f32[40,6144]{1,0:T(8,128)S(1)} %get-tuple-element.11, ...), channel_id=1, replica_groups=mesh['row'=4,'col'=8] {'row','col'}, use_global_device_ids=true, to_apply=%region_3.4 | all-reduce | flops 983040 | bytes 5898240 | tf_op jit(solution)/shard_map/psum | solution.py:24
  113.8 2.9 %pad_maximum_fusion.1 = bf16[160,6144]{1,0:T(8,128)(2,1)} fusion(bf16[40,6144]{1,0:T(8,128)(2,1)} %get-tuple-element.5, bf16[40,6144]{1,0:T(8,128)(2,1)} %get-tuple-element.6, bf16[40,6144]{1,0:T(8,128)(2,1)} %get-tuple-element.7, bf16[40,6144]{1,0:T(8,128)(2,1)} %get-tuple-element.8), kind=kLoop, calls=%fused_computation.2 | loop fusion | flops 7864320 | bytes 3932160 | tf_op jit(solution)/shard_map/concatenate | solution.py:26
  (3 shorter events, 0.0 us)
Async XLA Ops:
  0.0 1.1 copy-start
  0.0 5.4 %copy-start.2 = (bf16[384,6144]{1,0:T(8,128)(2,1)S(1)}, bf16[384,6144]{1,0:T(8,128)(2,1)}, u32[]{:S(2)}) copy-start(bf16[384,6144]{1,0:T(8,128)(2,1)} %param.7) | copy-start | bytes 14155780
  5.4 2.3 %copy-start.1 = (bf16[384,6144]{1,0:T(8,128)(2,1)S(1)}, bf16[384,6144]{1,0:T(8,128)(2,1)}, u32[]{:S(2)}) copy-start(bf16[384,6144]{1,0:T(8,128)(2,1)} %param.6) | copy-start | bytes 14155780
  5.4 2.3 %copy-start.4 = (bf16[384,48]{0,1:T(8,128)(2,1)S(1)}, bf16[384,48]{0,1:T(8,128)(2,1)}, u32[]{:S(2)}) copy-start(bf16[384,48]{0,1:T(8,128)(2,1)} %param.9) | copy-start | bytes 110596
  7.7 0.9 copy-start.3
  9.6 2.2 %copy-start.5 = (s32[160]{0:T(256)S(1)}, s32[160]{0:T(256)}, u32[]{:S(2)}) copy-start(s32[160]{0:T(256)} %param.11) | copy-start | bytes 1924
where the time goes:
time: 118 us; the launch traced here: 117 us
  blocking collectives  90.6 us (77%)
  local copies, waits for them, and re-layouts  11.1 us (9%)
  other arithmetic  7.78 us (7%)
  matrix products  7.13 us (6%)
    psum x1, blocking collectives, local(): summed = lax.psum(piece, ('row', 'col')).astype(jnp.bfloat16)  90.6 us
    gather x1, local copies, waits for them, and re-layouts, local(): ordered = jnp.take(stacked, bucket_order, axis=0)  7.44 us
    dot_general x1, matrix products, local(): pre = jnp.dot(normed, w_in, preferred_element_type=jnp.float32)  4.31 us
    concatenate x1, other arithmetic, local(): return jnp.concatenate(results, axis=0)  2.92 us
    select_n x2, other arithmetic, local(): ordered = jnp.take(stacked, bucket_order, axis=0)  2.7 us
    unnamed x12, local copies, waits for them, and re-layouts  2.46 us

commit v1 on v0

v1 whole, which is shorter than its diff:
```python
import functools

import jax
import jax.numpy as jnp
from jax import lax
from jax.experimental import pallas as pl
from jax.experimental.pallas import tpu as pltpu
from jax.sharding import PartitionSpec as P

MESH = pl.DeviceIdType.MESH
LAG = 2
F32, BF16 = jnp.float32, jnp.bfloat16


def round_up(a, b):
    return -(-a // b) * b


def plan(n_row, n_col, d, qw, hw):
    nx, nz = n_row // 2, 4
    ny = n_col // nz
    unit = 2 * ny * nz * 128
    dp = round_up(d, unit)
    chunks = dp // unit
    rows = (round_up(qw, 16 * nx), round_up(2 * hw, 16 * nx))
    return dict(nx=nx, ny=ny, nz=nz, dp=dp, t=chunks, rows=rows, ch=ny * nz * 128, cy=nz * 128, cz=128, qw=qw, hw=hw)


def kernel(p, normed, out_grad, w_in, hidden_grad, qkv_grad, out, nrm, ogr, in_sem, out_sem, own, snd0, rcv0, s1, s2q, s2m, s3, ra_q, ra_m, rb_q, rb_m, rc, acc_q, acc_m, acc2, obuf, ssem, rsem):
    nx, ny, nz, nt = p["nx"], p["ny"], p["nz"], p["t"]
    ch, cy, cz = p["ch"], p["cy"], p["cz"]
    qw, hw = p["qw"], p["hw"]
    rows = p["rows"]
    base = (0, rows[0])
    part = (rows[0] // nx, rows[1] // nx)
    ct = 2 * ch
    r, c = lax.axis_index("row"), lax.axis_index("col")
    ic, ix = lax.rem(r, 2), r // 2
    iy, iz = lax.rem(c, ny), c // ny
    partner = (ix * 2 + (1 - ic), c)
    xp = [(lax.rem(ix + d, nx) * 2 + ic, c) for d in range(nx)]
    yp = [(r, iz * ny + lax.rem(iy + d, ny)) for d in range(ny)]
    zp = [(r, lax.rem(iz + d, nz) * ny + iy) for d in range(nz)]

    loads = {}
    for name, src, dst in (("n", normed, nrm), ("o", out_grad, ogr)):
        for t in range(nt):
            cols = pl.ds(t * ct, ct)
            cp = pltpu.make_async_copy(src.at[:, cols], dst.at[:, cols], in_sem.at[len(loads)])
            cp.start()
            loads[name, t] = cp

    barrier = pltpu.get_barrier_semaphore()
    peers = [partner] + xp[1:] + yp[1:] + zp[1:]
    for dev in peers:
        pl.semaphore_signal(barrier, inc=1, device_id=dev, device_id_type=MESH)

    lhs_q = qkv_grad[...].astype(F32).T.astype(BF16)

    sent = []

    def send(src, dst, dev):
        i = len(sent)
        cp = pltpu.make_async_remote_copy(src_ref=src, dst_ref=dst, send_sem=ssem.at[i], recv_sem=rsem.at[i], device_id=dev, device_id_type=MESH)
        cp.start()
        sent.append(cp)
        return cp

    def m(v, k):
        return pl.multiple_of(v, k)

    other_off = m((1 - ic) * ch, 128)
    own_off = m(ic * ch, 128)
    flight = {}

    def dot(lhs, buf, off):
        return jnp.dot(lhs, buf[:, pl.ds(off, ch)], preferred_element_type=F32)

    def zero_tail(g, used, dst, cols):
        if rows[g] > used:
            dst[pl.ds(base[g] + used, rows[g] - used), cols] = jnp.zeros((rows[g] - used, ch), F32)

    def ship(g, t):
        region = (pl.ds(base[g], rows[g]), pl.ds(t * ch, ch))
        flight[g, t, 0] = [send(snd0.at[region], rcv0.at[region], partner)]

    pre = None

    def partial_q(t):
        cols = pl.ds(t * ch, ch)
        snd0[pl.ds(0, qw), cols] = dot(lhs_q, nrm, m(t * ct + other_off, 128))
        zero_tail(0, qw, snd0, cols)
        ship(0, t)
        own[pl.ds(0, qw), cols] = dot(lhs_q, nrm, m(t * ct + own_off, 128))
        zero_tail(0, qw, own, cols)

    def partial_m(t):
        cols = pl.ds(t * ch, ch)
        for dst, off in ((snd0, other_off), (own, own_off)):
            at = m(t * ct + off, 128)
            dst[pl.ds(base[1], hw), cols] = dot(lhs_in, nrm, at)
            dst[pl.ds(base[1] + hw, hw), cols] = dot(lhs_out, ogr, at)
            zero_tail(1, 2 * hw, dst, cols)
            if dst is snd0:
                ship(1, t)

    def wait(g, t, s):
        for cp in flight[g, t, s]:
            cp.wait_recv()

    def row_part(g, i):
        return pl.ds(m(i * part[g], 16), part[g])

    def stage1(g, t):
        wait(g, t, 0)
        region = (pl.ds(base[g], rows[g]), pl.ds(t * ch, ch))
        v = own[region] + rcv0[region]
        own[region] = v
        s1[region] = v.astype(BF16)
        cps = []
        if g == 0:
            for d in range(1, nx):
                src = s1.at[row_part(0, lax.rem(ix + d, nx)), pl.ds(t * ch, ch)]
                cps.append(send(src, ra_q.at[d - 1, :, pl.ds(t * ch, ch)], xp[d]))
        else:
            for d in range(1, ny):
                src = s1.at[pl.ds(base[1], rows[1]), pl.ds(m(t * ch + lax.rem(iy + d, ny) * cy, 128), cy)]
                cps.append(send(src, ra_m.at[d - 1, :, pl.ds(t * cy, cy)], yp[d]))
        flight[g, t, 1] = cps

    def stage2(g, t):
        wait(g, t, 1)
        cps = []
        if g == 0:
            cols = pl.ds(t * ch, ch)
            v = own[row_part(0, ix), cols]
            for d in range(1, nx):
                v = v + ra_q[d - 1, :, cols].astype(F32)
            acc_q[:, cols] = v
            s2q[:, cols] = v.astype(BF16)
            for d in range(1, ny):
                src = s2q.at[:, pl.ds(m(t * ch + lax.rem(iy + d, ny) * cy, 128), cy)]
                cps.append(send(src, rb_q.at[d - 1, :, pl.ds(t * cy, cy)], yp[d]))
        else:
            cols = pl.ds(t * cy, cy)
            v = own[pl.ds(base[1], rows[1]), pl.ds(m(t * ch + iy * cy, 128), cy)]
            for d in range(1, ny):
                v = v + ra_m[d - 1, :, cols].astype(F32)
            acc_m[:, cols] = v
            s2m[:, cols] = v.astype(BF16)
            for d in range(1, nx):
                src = s2m.at[row_part(1, lax.rem(ix + d, nx)), cols]
                cps.append(send(src, rb_m.at[d - 1, :, cols], xp[d]))
        flight[g, t, 2] = cps

    def stage3(g, t):
        wait(g, t, 2)
        cols = pl.ds(t * cy, cy)
        at = pl.ds(g * part[0], part[g])
        if g == 0:
            v = acc_q[:, pl.ds(m(t * ch + iy * cy, 128), cy)]
            for d in range(1, ny):
                v = v + rb_q[d - 1, :, cols].astype(F32)
        else:
            v = acc_m[row_part(1, ix), cols]
            for d in range(1, nx):
                v = v + rb_m[d - 1, :, cols].astype(F32)
        acc2[at, cols] = v
        s3[at, cols] = v.astype(BF16)
        cps = []
        for d in range(1, nz):
            src = s3.at[at, pl.ds(m(t * cy + lax.rem(iz + d, nz) * cz, 128), cz)]
            cps.append(send(src, rc.at[d - 1, at, pl.ds(t * cz, cz)], zp[d]))
        flight[g, t, 3] = cps

    def mine(g):
        return pl.ds(m(base[g] + ix * part[g], 16), part[g])

    def spread(region, devs):
        return [send(obuf.at[region], obuf.at[region], dev) for dev in devs]

    def stage4(g, t):
        wait(g, t, 3)
        at = pl.ds(g * part[0], part[g])
        v = acc2[at, pl.ds(m(t * cy + iz * cz, 128), cz)]
        for d in range(1, nz):
            v = v + rc[d - 1, at, pl.ds(t * cz, cz)].astype(F32)
        region = (mine(g), pl.ds(m(t * ct + own_off + iy * cy + iz * cz, 128), cz))
        obuf[region] = v.astype(BF16)
        flight[g, t, 4] = spread(region, zp[1:])

    def stage5(g, t):
        wait(g, t, 4)
        region = (mine(g), pl.ds(m(t * ct + own_off + iy * cy, 128), cy))
        flight[g, t, 5] = spread(region, (yp if g == 0 else xp)[1:])

    def stage6(g, t):
        wait(g, t, 5)
        if g == 0:
            flight[g, t, 6] = spread((mine(0), pl.ds(m(t * ct + own_off, 128), ch)), xp[1:])
        else:
            flight[g, t, 6] = spread((pl.ds(base[1], rows[1]), pl.ds(m(t * ct + own_off + iy * cy, 128), cy)), yp[1:])

    def stage7(g, t):
        wait(g, t, 6)
        flight[g, t, 7] = spread((pl.ds(base[g], rows[g]), pl.ds(m(t * ct + own_off, 128), ch)), [partner])

    outs = []

    def stage8(g, t):
        wait(g, t, 7)
        region = (pl.ds(base[g], rows[g]), pl.ds(t * ct, ct))
        cp = pltpu.make_async_copy(obuf.at[region], out.at[region], out_sem.at[g * nt + t])
        cp.start()
        outs.append(cp)

    stages = [None, stage1, stage2, stage3, stage4, stage5, stage6, stage7, stage8]

    for t in range(nt):
        loads["n", t].wait()
        if t == 0:
            pl.semaphore_wait(barrier, len(peers))
        partial_q(t)
        term = jnp.dot(nrm[:, t * ct : (t + 1) * ct], w_in[t * ct : (t + 1) * ct, :], preferred_element_type=F32)
        pre = term if pre is None else pre + term
    for t in range(nt):
        stage1(0, t)
    cdf = 0.5 * (1.0 + lax.erf(pre * 0.7071067811865476))
    pdf = jnp.exp(-0.5 * pre * pre) * 0.3989422804014327
    lhs_out = (pre * cdf).T.astype(BF16)
    lhs_in = (hidden_grad[...].astype(F32) * (cdf + pre * pdf)).T.astype(BF16)
    for t in range(nt):
        loads["o", t].wait()
        partial_m(t)
    for step in range(2, 9 + LAG):
        for t in range(nt):
            if step <= 8:
                stages[step](0, t)
            if 1 <= step - LAG + 1 <= 8:
                stages[step - LAG + 1](1, t)
    for cp in sent:
        cp.wait_send()
    for cp in outs:
        cp.wait()


def local(p, normed, out_grad, w_in, hidden_grad, qkv_grad, bucket_order):
    tok, d = normed.shape
    dp, nt, nx, ny, nz = p["dp"], p["t"], p["nx"], p["ny"], p["nz"]
    ch, cy, cz, rows = p["ch"], p["cy"], p["cz"], p["rows"]
    if dp > d:
        normed = jnp.pad(normed, ((0, 0), (0, dp - d)))
        out_grad = jnp.pad(out_grad, ((0, 0), (0, dp - d)))
        w_in = jnp.pad(w_in, ((0, dp - d), (0, 0)))
    total = sum(rows)
    part = (rows[0] // nx, rows[1] // nx)
    per_chunk = 2 + 2 * (nx - 1) + 2 * (ny - 1) + 2 * (nz - 1)
    copies = 2 * nt * per_chunk
    vmem = pl.BlockSpec(memory_space=pltpu.VMEM)
    hbm = pl.BlockSpec(memory_space=pl.ANY)
    gathered = pl.pallas_call(
        functools.partial(kernel, p),
        out_shape=jax.ShapeDtypeStruct((total, dp), BF16),
        in_specs=[hbm, hbm, vmem, vmem, vmem],
        out_specs=hbm,
        scratch_shapes=[
            pltpu.VMEM((tok, dp), BF16),
            pltpu.VMEM((tok, dp), BF16),
            pltpu.SemaphoreType.DMA((2 * nt,)),
            pltpu.SemaphoreType.DMA((2 * nt,)),
            pltpu.VMEM((total, nt * ch), F32),
            pltpu.VMEM((total, nt * ch), F32),
            pltpu.VMEM((total, nt * ch), F32),
            pltpu.VMEM((total, nt * ch), BF16),
            pltpu.VMEM((part[0], nt * ch), BF16),
            pltpu.VMEM((rows[1], nt * cy), BF16),
            pltpu.VMEM((sum(part), nt * cy), BF16),
            pltpu.VMEM((nx - 1, part[0], nt * ch), BF16),
            pltpu.VMEM((ny - 1, rows[1], nt * cy), BF16),
            pltpu.VMEM((ny - 1, part[0], nt * cy), BF16),
            pltpu.VMEM((nx - 1, part[1], nt * cy), BF16),
            pltpu.VMEM((nz - 1, sum(part), nt * cz), BF16),
            pltpu.VMEM((part[0], nt * ch), F32),
            pltpu.VMEM((rows[1], nt * cy), F32),
            pltpu.VMEM((sum(part), nt * cy), F32),
            pltpu.VMEM((total, dp), BF16),
            pltpu.SemaphoreType.DMA((copies,)),
            pltpu.SemaphoreType.DMA((copies,)),
        ],
        compiler_params=pltpu.CompilerParams(collective_id=0, has_side_effects=True, vmem_limit_bytes=60 * 2**20),
    )(normed, out_grad, w_in, hidden_grad, qkv_grad)
    order = jnp.where(bucket_order < p["qw"], bucket_order, bucket_order + (rows[0] - p["qw"]))
    pick = (order[:, None] == jnp.arange(total, dtype=jnp.int32)[None, :]).astype(BF16)
    return jnp.dot(pick, gathered[:, :d], preferred_element_type=F32).astype(BF16)


def solution(mesh):
    n_row, n_col = mesh.shape["row"], mesh.shape["col"]
    split = P(("row", "col"), None)

    def step(normed, out_grad, w_in, hidden_grad, qkv_grad, bucket_order):
        p = plan(n_row, n_col, normed.shape[1], qkv_grad.shape[1], w_in.shape[1])
        body = jax.shard_map(
            functools.partial(local, p),
            mesh=mesh,
            in_specs=(split, split, P(), split, split, P()),
            out_specs=P(),
            check_vma=False,
        )
        return body(normed, out_grad, w_in, hidden_grad, qkv_grad, bucket_order)

    return step
```

time: 118 us -> 56.8 us (0.48)
  blocking collectives: 90.6 us -> 0 us
  Pallas kernels: 0 us -> 47.5 us
  other arithmetic: 7.78 us -> 0 us
  local copies, waits for them, and re-layouts: 11.1 us -> 5.49 us
  matrix products: 7.13 us -> 3.53 us
    psum x1 -> x0, blocking collectives: 90.6 us -> none  [local(): summed = lax.psum(piece, ('row', 'col')).astype(jnp.bfloat16)]
    pallas_call x0 -> x1, Pallas kernels: none -> 47.5 us  [local(): pl.pallas_call(functools.partial(kernel, p), out_shape=jax.ShapeDtypeStru...]
    gather x1 -> x0, local copies, waits for them, and re-layouts: 7.44 us -> none  [local(): ordered = jnp.take(stacked, bucket_order, axis=0)]
    concatenate x2 -> x0, other arithmetic: 5.06 us -> none  [the longest x1 2.92 us: local(): return jnp.concatenate(results, axis=0)]
    dot_general x4 -> x1, matrix products: 7.13 us -> 3.53 us  [local(): jnp.dot(pick, gathered[:, :d], preferred_element_type=F32).astype(BF16)]
    unnamed x12 -> x5, local copies, waits for them, and re-layouts: 2.46 us -> 5.49 us
    select_n x2 -> x0, other arithmetic: 2.7 us -> none  [local(): ordered = jnp.take(stacked, bucket_order, axis=0)]
    slice x1 -> x0, local copies, waits for them, and re-layouts: 1.24 us -> none  [local(): piece = ordered[bucket * per_bucket:(bucket + 1) * per_bucket]]
where the time goes in v1:
time: 56.8 us; the launch traced here: 56.5 us
  Pallas kernels  47.5 us (84%)
  local copies, waits for them, and re-layouts  5.49 us (10%)
  matrix products  3.53 us (6%)
    pallas_call x1, Pallas kernels, local(): pl.pallas_call(functools.partial(kernel, p), out_shape=jax.ShapeDtypeStru...  47.5 us
    unnamed x5, local copies, waits for them, and re-layouts  5.49 us
    dot_general x1, matrix products, local(): jnp.dot(pick, gathered[:, :d], preferred_element_type=F32).astype(BF16)  3.53 us

profile of v1, /device:TPU:1, one launch (start us, length us, event | category | flops | bytes accessed | tf_op | source)
XLA Modules:
  0.0 56.5 jit_solution(2844409552151615081)
XLA Ops:
  0.0 1.5 %copy.8.hidden_grad = bf16[384,48]{1,0:T(8,128)(2,1)} copy(bf16[384,48]{0,1:T(8,128)(2,1)} %param.9) | data formatting | bytes 73728 | tf_op args[3]
  1.5 1.6 %copy.9.qkv_grad = bf16[384,64]{1,0:T(8,128)(2,1)} copy(bf16[384,64]{0,1:T(8,128)(2,1)} %param.10) | data formatting | bytes 98304 | tf_op args[4]
  3.1 2.4 %copy.7.w_in = bf16[6144,48]{1,0:T(8,128)(2,1)} copy(bf16[6144,48]{0,1:T(8,128)(2,1)} %param.8) | data formatting | bytes 1179648 | tf_op args[2]
  5.5 0.0 copy-start
  5.5 47.5 %shard_map.64 = bf16[160,6144]{1,0:T(8,128)(2,1)} custom-call(bf16[384,6144]{1,0:T(8,128)(2,1)} %normed.1, bf16[384,6144]{1,0:T(8,128)(2,1)} %out_grad.1, bf16[6144,48]{1,0:T(8,128)(2,1)} %copy.7.w_in, bf16[384,48]{1,0:T(8,128)(2,1)} %copy.8.hidden_grad, bf16[384,64]{1,0:T(8,128)(2,1)} %copy.9.qkv_grad), custom_call_target="tpu_custom_call" | custom-call | tf_op jit(solution)/shard_map/pallas_call | solution.py:261
  53.0 0.0 copy-done
  53.0 3.5 %convolution_convert_fusion = bf16[160,6144]{1,0:T(8,128)(2,1)} fusion(bf16[160,6144]{1,0:T(8,128)(2,1)} %shard_map.64, s32[160]{0:T(256)S(1)} %copy-done), kind=kOutput, calls=%fused_computation | convolution fusion | flops 315581440 | bytes 3932800 | tf_op jit(solution)/shard_map/dot_general | solution.py:294
Async XLA Ops:
  5.5 47.5 %copy-start = (s32[160]{0:T(256)S(1)}, s32[160]{0:T(256)}, u32[]{:S(2)}) copy-start(s32[160]{0:T(256)} %param.11) | copy-start | bytes 1924

commit v2 on v1

--- a/solution.py
+++ b/solution.py
@@ -8,7 +8,7 @@
 from jax.sharding import PartitionSpec as P
 
 MESH = pl.DeviceIdType.MESH
-LAG = 2
+LAG = 0
 F32, BF16 = jnp.float32, jnp.bfloat16
 
 
@@ -26,7 +26,7 @@
     return dict(nx=nx, ny=ny, nz=nz, dp=dp, t=chunks, rows=rows, ch=ny * nz * 128, cy=nz * 128, cz=128, qw=qw, hw=hw)
 
 
-def kernel(p, normed, out_grad, w_in, hidden_grad, qkv_grad, out, nrm, ogr, in_sem, out_sem, own, snd0, rcv0, s1, s2q, s2m, s3, ra_q, ra_m, rb_q, rb_m, rc, acc_q, acc_m, acc2, obuf, ssem, rsem):
+def kernel(p, normed, out_grad, w_hbm, hidden_hbm, qkv_hbm, out, nrm, ogr, w_in, hidden_grad, qkv_grad, in_sem, out_sem, own, snd0, rcv0, s1, s2q, s2m, s3, ra_q, ra_m, rb_q, rb_m, rc, acc_q, acc_m, acc2, obuf, ssem, rsem):
     nx, ny, nz, nt = p["nx"], p["ny"], p["nz"], p["t"]
     ch, cy, cz = p["ch"], p["cy"], p["cz"]
     qw, hw = p["qw"], p["hw"]
@@ -43,19 +43,25 @@
     zp = [(r, lax.rem(iz + d, nz) * ny + iy) for d in range(nz)]
 
     loads = {}
-    for name, src, dst in (("n", normed, nrm), ("o", out_grad, ogr)):
-        for t in range(nt):
-            cols = pl.ds(t * ct, ct)
-            cp = pltpu.make_async_copy(src.at[:, cols], dst.at[:, cols], in_sem.at[len(loads)])
-            cp.start()
-            loads[name, t] = cp
-
+
+    def load(key, src, dst):
+        loads[key] = pltpu.make_async_copy(src, dst, in_sem.at[len(loads)])
+        loads[key].start()
+
+    def load_cols(name, src, dst, t):
+        cols = pl.ds(t * ct, ct)
+        load((name, t), src.at[:, cols], dst.at[:, cols])
+
+    load("w", w_hbm, w_in)
+    for t in range(nt):
+        load_cols("n", normed, nrm, t)
+    load("h", hidden_hbm, hidden_grad)
+    load("q", qkv_hbm, qkv_grad)
     barrier = pltpu.get_barrier_semaphore()
     peers = [partner] + xp[1:] + yp[1:] + zp[1:]
     for dev in peers:
         pl.semaphore_signal(barrier, inc=1, device_id=dev, device_id_type=MESH)
 
-    lhs_q = qkv_grad[...].astype(F32).T.astype(BF16)
 
     sent = []
 
@@ -84,25 +90,15 @@
         region = (pl.ds(base[g], rows[g]), pl.ds(t * ch, ch))
         flight[g, t, 0] = [send(snd0.at[region], rcv0.at[region], partner)]
 
-    pre = None
-
-    def partial_q(t):
+    def partial(dst, off, t):
         cols = pl.ds(t * ch, ch)
-        snd0[pl.ds(0, qw), cols] = dot(lhs_q, nrm, m(t * ct + other_off, 128))
-        zero_tail(0, qw, snd0, cols)
-        ship(0, t)
-        own[pl.ds(0, qw), cols] = dot(lhs_q, nrm, m(t * ct + own_off, 128))
-        zero_tail(0, qw, own, cols)
-
-    def partial_m(t):
-        cols = pl.ds(t * ch, ch)
-        for dst, off in ((snd0, other_off), (own, own_off)):
-            at = m(t * ct + off, 128)
-            dst[pl.ds(base[1], hw), cols] = dot(lhs_in, nrm, at)
-            dst[pl.ds(base[1] + hw, hw), cols] = dot(lhs_out, ogr, at)
-            zero_tail(1, 2 * hw, dst, cols)
-            if dst is snd0:
-                ship(1, t)
+        at = m(t * ct + off, 128)
+        v = dot(lhs_n, nrm, at)
+        dst[pl.ds(0, qw), cols] = v[:qw]
+        dst[pl.ds(base[1], hw), cols] = v[qw:]
+        dst[pl.ds(base[1] + hw, hw), cols] = dot(lhs_out, ogr, at)
+        zero_tail(0, qw, dst, cols)
+        zero_tail(1, 2 * hw, dst, cols)
 
     def wait(g, t, s):
         for cp in flight[g, t, s]:
@@ -216,28 +212,34 @@
 
     stages = [None, stage1, stage2, stage3, stage4, stage5, stage6, stage7, stage8]
 
+    pre = None
     for t in range(nt):
         loads["n", t].wait()
         if t == 0:
-            pl.semaphore_wait(barrier, len(peers))
-        partial_q(t)
-        term = jnp.dot(nrm[:, t * ct : (t + 1) * ct], w_in[t * ct : (t + 1) * ct, :], preferred_element_type=F32)
+            loads["w"].wait()
+        load_cols("o", out_grad, ogr, t)
+        cols = slice(t * ct, (t + 1) * ct)
+        term = lax.dot_general(w_in[:, cols], nrm[:, cols], (((1,), (1,)), ((), ())), preferred_element_type=F32)
         pre = term if pre is None else pre + term
-    for t in range(nt):
-        stage1(0, t)
+    loads["h"].wait()
+    loads["q"].wait()
+    lhs_q = qkv_grad[...]
     cdf = 0.5 * (1.0 + lax.erf(pre * 0.7071067811865476))
     pdf = jnp.exp(-0.5 * pre * pre) * 0.3989422804014327
-    lhs_out = (pre * cdf).T.astype(BF16)
-    lhs_in = (hidden_grad[...].astype(F32) * (cdf + pre * pdf)).T.astype(BF16)
+    lhs_out = (pre * cdf).astype(BF16)
+    lhs_in = (hidden_grad[...].astype(F32) * (cdf + pre * pdf)).astype(BF16)
+    lhs_n = jnp.concatenate([lhs_q, lhs_in], axis=0)
+    pl.semaphore_wait(barrier, len(peers))
     for t in range(nt):
         loads["o", t].wait()
-        partial_m(t)
-    for step in range(2, 9 + LAG):
-        for t in range(nt):
-            if step <= 8:
-                stages[step](0, t)
-            if 1 <= step - LAG + 1 <= 8:
-                stages[step - LAG + 1](1, t)
+        partial(snd0, other_off, t)
+        ship(1, t)
+        ship(0, t)
+    for t in range(nt):
+        partial(own, own_off, t)
+    todo = [(s + LAG * (1 - g), 1 - g, t, s) for g in range(2) for t in range(nt) for s in range(1, 9)]
+    for _, q, t, s in sorted(todo, key=lambda e: (e[0], e[2], e[1])):
+        stages[s](1 - q, t)
     for cp in sent:
         cp.wait_send()
     for cp in outs:
@@ -260,13 +262,16 @@
     hbm = pl.BlockSpec(memory_space=pl.ANY)
     gathered = pl.pallas_call(
         functools.partial(kernel, p),
-        out_shape=jax.ShapeDtypeStruct((total, dp), BF16),
-        in_specs=[hbm, hbm, vmem, vmem, vmem],
-        out_specs=hbm,
+        out_shape=pltpu.VMEM((total, dp), BF16),
+        in_specs=[hbm] * 5,
+        out_specs=vmem,
         scratch_shapes=[
             pltpu.VMEM((tok, dp), BF16),
             pltpu.VMEM((tok, dp), BF16),
-            pltpu.SemaphoreType.DMA((2 * nt,)),
+            pltpu.VMEM((p["hw"], dp), BF16),
+            pltpu.VMEM((p["hw"], tok), BF16),
+            pltpu.VMEM((p["qw"], tok), BF16),
+            pltpu.SemaphoreType.DMA((2 * nt + 3,)),
             pltpu.SemaphoreType.DMA((2 * nt,)),
             pltpu.VMEM((total, nt * ch), F32),
             pltpu.VMEM((total, nt * ch), F32),
@@ -287,8 +292,8 @@
             pltpu.SemaphoreType.DMA((copies,)),
             pltpu.SemaphoreType.DMA((copies,)),
         ],
-        compiler_params=pltpu.CompilerParams(collective_id=0, has_side_effects=True, vmem_limit_bytes=60 * 2**20),
-    )(normed, out_grad, w_in, hidden_grad, qkv_grad)
+        compiler_params=pltpu.CompilerParams(collective_id=0, has_side_effects=True, vmem_limit_bytes=48 * 2**20),
+    )(normed, out_grad, w_in.T, hidden_grad.T, qkv_grad.T)
     order = jnp.where(bucket_order < p["qw"], bucket_order, bucket_order + (rows[0] - p["qw"]))
     pick = (order[:, None] == jnp.arange(total, dtype=jnp.int32)[None, :]).astype(BF16)
     return jnp.dot(pick, gathered[:, :d], preferred_element_type=F32).astype(BF16)

time: 56.8 us -> 46.6 us (0.82)
  Pallas kernels: 47.5 us -> 41.7 us
  local copies, waits for them, and re-layouts: 5.49 us -> 2.63 us
  matrix products: 3.53 us -> 1.99 us
    pallas_call x1, Pallas kernels: 47.5 us -> 41.7 us  [local(): pl.pallas_call(functools.partial(kernel, p), out_shape=pltpu.VMEM((total,...]
    unnamed x5 -> x8, local copies, waits for them, and re-layouts: 5.49 us -> 2.63 us
    dot_general x1, matrix products: 3.53 us -> 1.99 us  [local(): jnp.dot(pick, gathered[:, :d], preferred_element_type=F32).astype(BF16)]
where the time goes in v2:
time: 46.6 us; the launch traced here: 46.3 us
  Pallas kernels  41.7 us (89%)
  local copies, waits for them, and re-layouts  2.63 us (6%)
  matrix products  1.99 us (4%)
    pallas_call x1, Pallas kernels, local(): pl.pallas_call(functools.partial(kernel, p), out_shape=pltpu.VMEM((total,...  41.7 us
    unnamed x8, local copies, waits for them, and re-layouts  2.63 us
    dot_general x1, matrix products, local(): jnp.dot(pick, gathered[:, :d], preferred_element_type=F32).astype(BF16)  1.99 us

profile of v2, /device:TPU:1, one launch (start us, length us, event | category | flops | bytes accessed | tf_op | source)
XLA Modules:
  0.0 46.3 jit_solution(5398829127831852473)
XLA Ops:
  0.0 0.0 copy-start
  0.0 1.1 %copy-done = bf16[6144,48]{0,1:T(8,128)(2,1)S(1)} copy-done((bf16[6144,48]{0,1:T(8,128)(2,1)S(1)}, bf16[6144,48]{0,1:T(8,128)(2,1)}, u32[]{:S(2)}) %copy-start) | copy-done | bytes 589848
  1.1 0.0 copy-start.1
  1.1 0.8 %copy-done.1 = bf16[384,64]{0,1:T(8,128)(2,1)S(1)} copy-done((bf16[384,64]{0,1:T(8,128)(2,1)S(1)}, bf16[384,64]{0,1:T(8,128)(2,1)}, u32[]{:S(2)}) %copy-start.1) | copy-done | bytes 49176
  1.9 0.0 copy-start.2
  1.9 0.8 %copy-done.2 = bf16[384,48]{0,1:T(8,128)(2,1)S(1)} copy-done((bf16[384,48]{0,1:T(8,128)(2,1)S(1)}, bf16[384,48]{0,1:T(8,128)(2,1)}, u32[]{:S(2)}) %copy-start.2) | copy-done | bytes 36888
  2.6 0.0 copy-start.3
  2.6 41.7 %shard_map.64 = bf16[160,6144]{1,0:T(8,128)(2,1)S(1)} custom-call(bf16[384,6144]{1,0:T(8,128)(2,1)} %normed.1, bf16[384,6144]{1,0:T(8,128)(2,1)} %out_grad.1, bf16[48,6144]{1,0:T(8,128)(2,1)S(1)} %bitcast.4, bf16[48,384]{1,0:T(8,128)(2,1)S(1)} %bitcast.6, bf16[64,384]{1,0:T(8,128)(2,1)S(1)} %bitcast.5), custom_call_target="tpu_custom_call" | custom-call | tf_op jit(solution)/shard_map/pallas_call | solution.py:263
  44.3 0.0 copy-done.3
  44.3 2.0 %convolution_convert_fusion = bf16[160,6144]{1,0:T(8,128)(2,1)} fusion(bf16[160,6144]{1,0:T(8,128)(2,1)S(1)} %shard_map.64, s32[160]{0:T(256)S(1)} %copy-done.3), kind=kOutput, calls=%fused_computation | convolution fusion | flops 315581440 | bytes 3932800 | tf_op jit(solution)/shard_map/dot_general | solution.py:299
Async XLA Ops:
  0.0 1.1 %copy-start = (bf16[6144,48]{0,1:T(8,128)(2,1)S(1)}, bf16[6144,48]{0,1:T(8,128)(2,1)}, u32[]{:S(2)}) copy-start(bf16[6144,48]{0,1:T(8,128)(2,1)} %param.8) | copy-start | bytes 1769476
  1.1 0.8 %copy-start.1 = (bf16[384,64]{0,1:T(8,128)(2,1)S(1)}, bf16[384,64]{0,1:T(8,128)(2,1)}, u32[]{:S(2)}) copy-start(bf16[384,64]{0,1:T(8,128)(2,1)} %param.10) | copy-start | bytes 147460
  1.9 0.8 %copy-start.2 = (bf16[384,48]{0,1:T(8,128)(2,1)S(1)}, bf16[384,48]{0,1:T(8,128)(2,1)}, u32[]{:S(2)}) copy-start(bf16[384,48]{0,1:T(8,128)(2,1)} %param.9) | copy-start | bytes 110596
  2.6 41.7 %copy-start.3 = (s32[160]{0:T(256)S(1)}, s32[160]{0:T(256)}, u32[]{:S(2)}) copy-start(s32[160]{0:T(256)} %param.11) | copy-start | bytes 1924

commit v3 on v2

--- a/solution.py
+++ b/solution.py
@@ -84,7 +84,7 @@
 
     def zero_tail(g, used, dst, cols):
         if rows[g] > used:
-            dst[pl.ds(base[g] + used, rows[g] - used), cols] = jnp.zeros((rows[g] - used, ch), F32)
+            dst[pl.ds(base[g] + used, rows[g] - used), cols] = jnp.zeros((rows[g] - used, ch), dst.dtype)
 
     def ship(g, t):
         region = (pl.ds(base[g], rows[g]), pl.ds(t * ch, ch))
@@ -94,9 +94,9 @@
         cols = pl.ds(t * ch, ch)
         at = m(t * ct + off, 128)
         v = dot(lhs_n, nrm, at)
-        dst[pl.ds(0, qw), cols] = v[:qw]
-        dst[pl.ds(base[1], hw), cols] = v[qw:]
-        dst[pl.ds(base[1] + hw, hw), cols] = dot(lhs_out, ogr, at)
+        dst[pl.ds(0, qw), cols] = v[:qw].astype(dst.dtype)
+        dst[pl.ds(base[1], hw), cols] = v[qw:].astype(dst.dtype)
+        dst[pl.ds(base[1] + hw, hw), cols] = dot(lhs_out, ogr, at).astype(dst.dtype)
         zero_tail(0, qw, dst, cols)
         zero_tail(1, 2 * hw, dst, cols)
 
@@ -110,7 +110,7 @@
     def stage1(g, t):
         wait(g, t, 0)
         region = (pl.ds(base[g], rows[g]), pl.ds(t * ch, ch))
-        v = own[region] + rcv0[region]
+        v = own[region] + rcv0[region].astype(F32)
         own[region] = v
         s1[region] = v.astype(BF16)
         cps = []
@@ -274,8 +274,8 @@
             pltpu.SemaphoreType.DMA((2 * nt + 3,)),
             pltpu.SemaphoreType.DMA((2 * nt,)),
             pltpu.VMEM((total, nt * ch), F32),
-            pltpu.VMEM((total, nt * ch), F32),
-            pltpu.VMEM((total, nt * ch), F32),
+            pltpu.VMEM((total, nt * ch), BF16),
+            pltpu.VMEM((total, nt * ch), BF16),
             pltpu.VMEM((total, nt * ch), BF16),
             pltpu.VMEM((part[0], nt * ch), BF16),
             pltpu.VMEM((rows[1], nt * cy), BF16),
@@ -292,7 +292,7 @@
             pltpu.SemaphoreType.DMA((copies,)),
             pltpu.SemaphoreType.DMA((copies,)),
         ],
-        compiler_params=pltpu.CompilerParams(collective_id=0, has_side_effects=True, vmem_limit_bytes=48 * 2**20),
+        compiler_params=pltpu.CompilerParams(collective_id=0, has_side_effects=True, vmem_limit_bytes=67043328 - 4 * total * dp),
     )(normed, out_grad, w_in.T, hidden_grad.T, qkv_grad.T)
     order = jnp.where(bucket_order < p["qw"], bucket_order, bucket_order + (rows[0] - p["qw"]))
     pick = (order[:, None] == jnp.arange(total, dtype=jnp.int32)[None, :]).astype(BF16)

time: 46.6 us -> 43.3 us (0.929)
  local copies, waits for them, and re-layouts: 2.63 us -> 0.01 us
  Pallas kernels: 41.7 us -> 41.1 us
    unnamed x8 -> x2, local copies, waits for them, and re-layouts: 2.63 us -> 0.01 us
    pallas_call x1, Pallas kernels: 41.7 us -> 41.1 us  [local(): pl.pallas_call(functools.partial(kernel, p), out_shape=pltpu.VMEM((total,...]
where the time goes in v3:
time: 43.3 us; the launch traced here: 43.1 us
  Pallas kernels  41.1 us (95%)
  matrix products  1.99 us (5%)
    pallas_call x1, Pallas kernels, local(): pl.pallas_call(functools.partial(kernel, p), out_shape=pltpu.VMEM((total,...  41.1 us
    dot_general x1, matrix products, local(): jnp.dot(pick, gathered[:, :d], preferred_element_type=F32).astype(BF16)  1.99 us

profile of v3, /device:TPU:1, one launch (start us, length us, event | category | flops | bytes accessed | tf_op | source)
XLA Modules:
  0.0 43.1 jit_solution(14105259432997034416)
XLA Ops:
  0.0 0.0 copy-start
  0.0 41.1 %shard_map.64 = bf16[160,6144]{1,0:T(8,128)(2,1)S(1)} custom-call(bf16[384,6144]{1,0:T(8,128)(2,1)} %normed.1, bf16[384,6144]{1,0:T(8,128)(2,1)} %out_grad.1, bf16[48,6144]{1,0:T(8,128)(2,1)} %bitcast.4, bf16[48,384]{1,0:T(8,128)(2,1)} %bitcast.6, bf16[64,384]{1,0:T(8,128)(2,1)} %bitcast.5), custom_call_target="tpu_custom_call" | custom-call | tf_op jit(solution)/shard_map/pallas_call | solution.py:263
  41.1 0.0 copy-done
  41.1 2.0 %convolution_convert_fusion = bf16[160,6144]{1,0:T(8,128)(2,1)} fusion(bf16[160,6144]{1,0:T(8,128)(2,1)S(1)} %shard_map.64, s32[160]{0:T(256)S(1)} %copy-done), kind=kOutput, calls=%fused_computation | convolution fusion | flops 315581440 | bytes 3932800 | tf_op jit(solution)/shard_map/dot_general | solution.py:299
Async XLA Ops:
  0.0 41.1 %copy-start = (s32[160]{0:T(256)S(1)}, s32[160]{0:T(256)}, u32[]{:S(2)}) copy-start(s32[160]{0:T(256)} %param.11) | copy-start | bytes 1924
